TPU v7x, 32 devices: a whole 2x2x4 slice. The times are simulated.
32 devices in a mesh: blk: 32 (over z, y, x, core).
Axes of the slice: x: 2, y: 2, z: 4, core: 2. Of those that a mesh axis runs over, the one named last changes fastest.
Arguments:
- frames: float32 [128, 128, 1280], P('blk'), may hold values from -6 to 6
- widths: float32 [128], replicated, may hold values from 2 to 12
- kernel: float32 [3, 3], replicated, may hold values from -3 to 3
Outputs:
- filtered: float32 [128, 128, 1280], P(None, 'blk')
All inputs are finite; a program needn't handle non-finite values.
Results may differ from a plain program's by a relative error of at most 0.00007.
Values sent between devices are 32-bit elements; how exact they have to be, the bound alone decides.
A program may use at most 64 MiB of HBM per device.

v0:
```python
import jax
import jax.numpy as jnp
from jax import lax
from jax.sharding import PartitionSpec as P

BAND = 24


def temporal_matrix(widths, length):
    steps = jnp.arange(length, dtype=jnp.int32)
    offset = (steps[:, None] - steps[None, :]).astype(jnp.float32)
    inside = jnp.abs(offset) <= BAND
    spread = widths[:, None]
    weights = jnp.where(inside, jnp.exp(-offset * offset / (2.0 * spread * spread)), 0.0)
    return weights / jnp.sum(weights, axis=1, keepdims=True)


def stencil(padded, kernel):
    rows_out = padded.shape[1] - 2
    columns = padded.shape[2]
    widened = jnp.pad(padded, ((0, 0), (0, 0), (1, 1)))
    summed = jnp.zeros((padded.shape[0], rows_out, columns), jnp.float32)
    for row_off in range(3):
        for col_off in range(3):
            summed = (
                summed
                + kernel[row_off, col_off]
                * widened[:, row_off : row_off + rows_out, col_off : col_off + columns]
            )
    return summed


def local(frames, widths, kernel):
    weights = temporal_matrix(widths, widths.shape[0])
    local_filtered = stencil(jnp.pad(frames, ((0, 0), (1, 1), (0, 0))), kernel)
    return jnp.einsum(
        "ts,srw->trw",
        weights,
        lax.all_to_all(local_filtered, "blk", split_axis=1, concat_axis=0, tiled=True),
        precision=lax.Precision.HIGHEST,
    )


def solution(mesh):
    return jax.shard_map(
        local,
        mesh=mesh,
        in_specs=(P("blk", None, None), P(), P()),
        out_specs=P(None, "blk", None),
        check_vma=False,
    )
```

profile of v0, /device:TPU:0, one launch (start us, length us, event | category | flops | bytes accessed | tf_op | source)
XLA Modules:
  0.0 102.4 jit_solution(13410759657057529813)
XLA Ops:
  0.0 1.7 %fusion.13 = (f32[1,1]{1,0:T(1,128)}, f32[1,1]{1,0:T(1,128)}, f32[1,1]{1,0:T(1,128)}, f32[1,1]{1,0:T(1,128)}, f32[1,1]{1,0:T(1,128)}, /*index=5*/f32[1,1]{1,0:T(...) fusion(f32[3,3]{1,0:T(4,128)} %param.5), kind=kLoop, calls=%fused_computation.18 | loop fusion | bytes 72 | tf_op jit(solution)/shard_map/slice | solution.py:27
  1.7 3.4 %copy.6 = f32[4,128,1280]{2,0,1:T(4,128)S(1)} copy(f32[4,128,1280]{2,1,0:T(8,128)} %param.3) | data formatting | bytes 5242880 | tf_op args[0]
  5.1 0.0 copy-start
  5.1 0.5 pad.8
  5.6 1.3 %copy-done = f32[4,128,1280]{2,1,0:T(8,128)S(1)} copy-done((f32[4,128,1280]{2,1,0:T(8,128)S(1)}, f32[4,128,1280]{2,1,0:T(8,128)}, u32[]{:S(2)}) %copy-start) | copy-done | bytes 2621464
  6.9 17.9 %multiply_add_fusion = f32[4,128,1280]{2,0,1:T(4,128)} fusion(f32[4,130,1280]{2,0,1:T(4,128)S(1)} %pad.8, f32[]{:T(128)} %bitcast.9, f32[]{:T(128)} %bitcast.8, f32[]{:T(128)} %bitcast.7, f32[]{:T(128)} %bitcast.6, f32[]{:T(128)} %bitcast.5, f32[]{:T(128)} %bitcast.4, f32[]{:T(128)} %bitcast.3, f32[]{:T(128)} %bitcast.2, f32[]{:T(128)} %bitcast.1, ...), kind=kLoop, calls=%fused_computation.1 | loop fusion | flops 11141120 | bytes 13148196 | tf_op jit(solution)/shard_map/add | solution.py:26
  24.8 0.0 copy-start.1
  24.8 7.3 %all-to-all-start = ((f32[4,128,1280]{2,0,1:T(4,128)}), f32[4,128,1280]{2,0,1:T(4,128)S(1)}, u32[]{:S(2)}, u32[]{:S(2)}) async-start(f32[4,128,1280]{2,0,1:T(4,128)} %multiply_add_fusion), calls=%async_computation | async-start | bytes 5242880 | tf_op jit(solution)/shard_map/all_to_all | solution.py:39
  32.1 0.0 copy-done.1
  32.2 0.2 fusion.10
  32.3 59.9 %all-to-all-done = f32[4,128,1280]{2,0,1:T(4,128)S(1)} async-done(((f32[4,128,1280]{2,0,1:T(4,128)}), f32[4,128,1280]{2,0,1:T(4,128)S(1)}, u32[]{:S(2)}, u32[]{:S(2)}) %all-to-all-start) | async-done | bytes 2621472 | tf_op jit(solution)/shard_map/all_to_all | solution.py:39
  92.2 1.7 %copy.12 = f32[4,32,4,1280]{3,0,1,2:T(4,128)} copy(f32[4,32,4,1280]{3,0,2,1:T(4,128)S(1)} %bitcast.19) | data formatting | bytes 5242880 | tf_op jit(solution)/shard_map/all_to_all | solution.py:39
  93.9 2.8 %all_to_all.16 = f32[128,4,1280]{2,0,1:T(8,128)S(1)} reshape(f32[32,4,4,1280]{3,1,0,2:T(4,128)} %bitcast.20) | data formatting | bytes 5242880 | tf_op jit(solution)/shard_map/all_to_all | solution.py:39
  96.7 2.5 %fusion.5 = f32[128,4,1280]{2,0,1:T(8,128)S(1)} fusion(f32[128,4,1280]{2,0,1:T(8,128)S(1)} %all_to_all.16, f32[128]{0:T(128)S(1)} %fusion.10, f32[128]{0:T(128)S(1)} %multiply_multiply_fusion), kind=kOutput, calls=%fused_computation.9 | convolution fusion | flops 1006780416 | bytes 5243904 | tf_op jit(solution)/shard_map/ts,srw->trw/dot_general | solution.py:36
  99.2 3.2 %copy.9 = f32[128,4,1280]{2,1,0:T(4,128)} copy(f32[128,4,1280]{2,0,1:T(8,128)S(1)} %fusion.5) | data formatting | bytes 5242880 | tf_op jit(solution)/shard_map/ts,srw->trw/dot_general | solution.py:36
  (1 shorter events, 0.0 us)
Async XLA Ops:
  5.1 1.7 %copy-start = (f32[4,128,1280]{2,1,0:T(8,128)S(1)}, f32[4,128,1280]{2,1,0:T(8,128)}, u32[]{:S(2)}) copy-start(f32[4,128,1280]{2,1,0:T(8,128)} %param.3) | copy-start | bytes 7864324
  24.8 7.3 %copy-start.1 = (f32[128]{0:T(128)S(1)}, f32[128]{0:T(128)}, u32[]{:S(2)}) copy-start(f32[128]{0:T(128)} %param.4) | copy-start | bytes 1540
  24.8 67.4 %all-to-all-start = ((f32[4,128,1280]{2,0,1:T(4,128)}), f32[4,128,1280]{2,0,1:T(4,128)S(1)}, u32[]{:S(2)}, u32[]{:S(2)}) async-start(f32[4,128,1280]{2,0,1:T(4,128)} %multiply_add_fusion), calls=%async_computation | async-start | bytes 5242880 | tf_op jit(solution)/shard_map/all_to_all | solution.py:39
where the time goes:
time: 103 us; the launch traced here: 102 us
  waiting for transfers between devices  59.9 us (58%)
  other arithmetic  18.1 us (18%)
  local copies, waits for them, and re-layouts  14.5 us (14%)
  starting transfers between devices  7.33 us (7%)
  matrix products  2.49 us (2%)
    all_to_all x1, waiting for transfers between devices, local(): lax.all_to_all(local_filtered, 'blk', split_axis=1, concat_axis=0, tiled=...  59.9 us
    add x1, other arithmetic, stencil(): summed + kernel[row_off, col_off] * widened[:, row_off:row_off + rows_out...  17.9 us
    all_to_all x1, starting transfers between devices, local(): lax.all_to_all(local_filtered, 'blk', split_axis=1, concat_axis=0, tiled=...  7.33 us
    unnamed x5, local copies, waits for them, and re-layouts  4.7 us
    all_to_all x2, local copies, waits for them, and re-layouts, local(): lax.all_to_all(local_filtered, 'blk', split_axis=1, concat_axis=0, tiled=...  4.49 us
    dot_general x1, local copies, waits for them, and re-layouts, local(): jnp.einsum('ts,srw->trw', weights, lax.all_to_all(local_filtered, 'blk',...  3.18 us
    dot_general x1, matrix products, local(): jnp.einsum('ts,srw->trw', weights, lax.all_to_all(local_filtered, 'blk',...  2.49 us
  transfers between devices with their start and end apart: 1, of which 1 were waited for; matrix products, arithmetic and copies ran while one was open for 0% of the time, Pallas kernels for 0%

commit v1 on v0

--- a/solution.py
+++ b/solution.py
@@ -36,7 +36,12 @@
     return jnp.einsum(
         "ts,srw->trw",
         weights,
-        lax.all_to_all(local_filtered, "blk", split_axis=1, concat_axis=0, tiled=True),
+        jnp.concatenate(
+            lax.all_to_all(
+                jnp.stack(jnp.split(local_filtered, lax.axis_size("blk"), axis=1)), "blk", 0, 0
+            ),
+            axis=0,
+        ),
         precision=lax.Precision.HIGHEST,
     )
 

time: 103 us -> 109 us (1.058)
  local copies, waits for them, and re-layouts: 14.5 us -> 28.2 us
  other arithmetic: 18.1 us -> 10.7 us
    unnamed x5 -> x35, local copies, waits for them, and re-layouts: 4.7 us -> 20.6 us
    add x1, other arithmetic: 17.9 us -> 10.5 us  [stencil(): summed + kernel[row_off, col_off] * widened[:, row_off:row_off + rows_out...]
    all_to_all x2 -> x0, local copies, waits for them, and re-layouts: 4.49 us -> none  [local(): lax.all_to_all(local_filtered, 'blk', split_axis=1, concat_axis=0, tiled=...]
    pad x1, local copies, waits for them, and re-layouts: 0.46 us -> 2.07 us  [local(): local_filtered = stencil(jnp.pad(frames, ((0, 0), (1, 1), (0, 0))), kernel)]
where the time goes in v1:
time: 109 us
  waiting for transfers between devices  59.9 us (55%)
  local copies, waits for them, and re-layouts  28.2 us (26%)
  other arithmetic  10.7 us (10%)
  starting transfers between devices  7.33 us (7%)
  matrix products  2.69 us (2%)
    all_to_all x1, waiting for transfers between devices, local(): lax.all_to_all(jnp.stack(jnp.split(local_filtered, lax.axis_size('blk'),...  59.9 us
    unnamed x35, local copies, waits for them, and re-layouts  20.6 us
    add x1, other arithmetic, stencil(): summed + kernel[row_off, col_off] * widened[:, row_off:row_off + rows_out...  10.5 us
    all_to_all x1, starting transfers between devices, local(): lax.all_to_all(jnp.stack(jnp.split(local_filtered, lax.axis_size('blk'),...  7.33 us
    dot_general x1, local copies, waits for them, and re-layouts, local(): jnp.einsum('ts,srw->trw', weights, jnp.concatenate(lax.all_to_all(jnp.sta...  3.18 us
    dot_general x1, matrix products, local(): jnp.einsum('ts,srw->trw', weights, jnp.concatenate(lax.all_to_all(jnp.sta...  2.69 us
  transfers between devices with their start and end apart: 1, of which 1 were waited for; matrix products, arithmetic and copies ran while one was open for 0% of the time, Pallas kernels for 0%

profile of v1, /device:TPU:0, one launch (start us, length us, event | category | flops | bytes accessed | tf_op | source)
XLA Modules:
  0.0 108.8 jit_solution(1806041078435849632)
XLA Ops:
  0.0 1.7 %fusion.58 = (f32[1,1]{1,0:T(1,128)}, f32[1,1]{1,0:T(1,128)}, f32[1,1]{1,0:T(1,128)}, f32[1,1]{1,0:T(1,128)}, f32[1,1]{1,0:T(1,128)}, /*index=5*/f32[1,1]{1,0:T(...) fusion(f32[3,3]{1,0:T(4,128)} %param.5), kind=kLoop, calls=%fused_computation.98 | loop fusion | bytes 72 | tf_op jit(solution)/shard_map/slice | solution.py:27
  1.7 2.1 %pad.8 = f32[4,130,1280]{2,1,0:T(8,128)S(1)} pad(f32[4,128,1280]{2,1,0:T(8,128)} %param.3, f32[]{:T(128)} %constant.2.clone.1), padding=0_0x1_1x0_0 | pad | bytes 5283844 | tf_op jit(solution)/shard_map/jit(_pad)/pad | solution.py:35
  4.2 10.5 %fusion.8 = f32[4,128,1280]{2,1,0:T(8,128)S(1)} fusion(f32[4,130,1280]{2,1,0:T(8,128)S(1)} %pad.8, f32[4,128,1280]{2,1,0:T(8,128)S(1)} %copy-done, f32[]{:T(128)} %bitcast.9, f32[]{:T(128)} %bitcast.8, f32[]{:T(128)} %bitcast.7, f32[]{:T(128)} %bitcast.6, f32[]{:T(128)} %bitcast.5, f32[]{:T(128)} %bitcast.4, f32[]{:T(128)} %bitcast.3, f32[]{:T(128)} %bitcast.2, ...), kind=kLoop, calls=%fused_computation.14 | loop fusion | flops 11141120 | bytes 13271076 | tf_op jit(solution)/shard_map/add | solution.py:26
  14.7 0.6 fusion.47
  15.3 0.7 fusion.46
  16.0 0.6 fusion.45
  16.6 0.7 fusion.44
  17.3 0.6 fusion.43
  17.9 0.7 fusion.42
  18.6 0.6 fusion.41
  19.2 0.7 fusion.40
  19.9 0.6 fusion.39
  20.5 0.7 fusion.38
  21.2 0.6 fusion.37
  21.8 0.7 fusion.36
  22.5 0.6 fusion.35
  23.1 0.7 fusion.34
  23.8 0.6 fusion.33
  24.4 0.7 fusion.32
  25.1 0.6 fusion.31
  25.7 0.7 fusion.30
  27.0 0.7 fusion.28
  28.3 0.7 fusion.26
  29.6 0.7 fusion.24
  30.9 0.7 fusion.22
  32.2 0.7 fusion.20
  33.5 0.7 fusion.18
  34.8 0.7 fusion.16
  35.5 7.3 %all-to-all-start = ((f32[32,4,4,1280]{3,2,1,0:T(4,128)}), f32[32,4,4,1280]{3,2,1,0:T(4,128)S(1)}, u32[]{:S(2)}, u32[]{:S(2)}) async-start(f32[32,4,4,1280]{3,2,1,0:T(4,128)} %fusion.16), calls=%async_computation | async-start | bytes 5242880 | tf_op jit(solution)/shard_map/all_to_all | solution.py:40
  43.0 59.9 %all-to-all-done = f32[32,4,4,1280]{3,2,1,0:T(4,128)S(1)} async-done(((f32[32,4,4,1280]{3,2,1,0:T(4,128)}), f32[32,4,4,1280]{3,2,1,0:T(4,128)S(1)}, u32[]{:S(2)}, u32[]{:S(2)}) %all-to-all-start) | async-done | bytes 2621472 | tf_op jit(solution)/shard_map/all_to_all | solution.py:40
  102.9 2.7 %fusion.14 = f32[128,4,1280]{2,0,1:T(8,128)S(1)} fusion(f32[128,4,1280]{2,1,0:T(4,128)S(1)} %bitcast.141, f32[128]{0:T(128)S(1)} %fusion.55, f32[128]{0:T(128)S(1)} %multiply_multiply_fusion), kind=kOutput, calls=%fused_computation.20 | convolution fusion | flops 1006780416 | bytes 5243904 | tf_op jit(solution)/shard_map/ts,srw->trw/dot_general | solution.py:36
  105.6 3.2 %copy.5 = f32[128,4,1280]{2,1,0:T(4,128)} copy(f32[128,4,1280]{2,0,1:T(8,128)S(1)} %fusion.14) | data formatting | bytes 5242880 | tf_op jit(solution)/shard_map/ts,srw->trw/dot_general | solution.py:36
  (13 shorter events, 5.2 us)
Async XLA Ops:
  1.7 2.5 %copy-start = (f32[4,128,1280]{2,1,0:T(8,128)S(1)}, f32[4,128,1280]{2,1,0:T(8,128)}, u32[]{:S(2)}) copy-start(f32[4,128,1280]{2,1,0:T(8,128)} %param.3) | copy-start | bytes 7864324
  35.5 7.3 %copy-start.1 = (f32[128]{0:T(128)S(1)}, f32[128]{0:T(128)}, u32[]{:S(2)}) copy-start(f32[128]{0:T(128)} %param.4) | copy-start | bytes 1540
  35.5 67.4 %all-to-all-start = ((f32[32,4,4,1280]{3,2,1,0:T(4,128)}), f32[32,4,4,1280]{3,2,1,0:T(4,128)S(1)}, u32[]{:S(2)}, u32[]{:S(2)}) async-start(f32[32,4,4,1280]{3,2,1,0:T(4,128)} %fusion.16), calls=%async_computation | async-start | bytes 5242880 | tf_op jit(solution)/shard_map/all_to_all | solution.py:40
